TPU v7x, 32 devices: a whole 2x2x4 slice. The times are simulated.
32 devices in a mesh: rep: 4 (over x, y), pp: 8 (over z, core).
Axes of the slice: x: 2, y: 2, z: 4, core: 2. Of those that a mesh axis runs over, the one named last changes fastest.
Arguments:
- x: bfloat16 [64, 512, 512], P('rep'), parts along dimension 0
- dy: bfloat16 [64, 512, 512], P('rep'), parts along dimension 0
- w_gate: bfloat16 [8, 512, 1536], P('pp')
- w_up: bfloat16 [8, 512, 1536], P('pp')
- w_down: bfloat16 [8, 1536, 512], P('pp')
Outputs:
- output 1: bfloat16 [32, 512, 1536], P(('rep', 'pp')), parts along dimension 0
- output 2: bfloat16 [32, 512, 1536], P(('rep', 'pp')), parts along dimension 0
- output 3: bfloat16 [32, 1536, 512], P(('rep', 'pp')), parts along dimension 0
There are 4 independent parts. A program takes and returns all parts, laid end to end along the dimension named above; an argument that names none is the same for every part.
All inputs are finite; a program needn't handle non-finite values.
Results may differ from a plain program's by a relative error of at most 0.0282.
Values are sent between devices in bfloat16 or wider.
A program may use at most 2 GiB of HBM per device.

v0:
```python
import jax
import jax.numpy as jnp
from jax import lax
from jax.sharding import PartitionSpec as P

NAMES = ("w_gate", "w_up", "w_down")


def matmul(a, w):
    return jnp.dot(a, w, preferred_element_type=jnp.float32).astype(jnp.bfloat16)


def normed(h):
    wide = h.astype(jnp.float32)
    scale = lax.rsqrt(jnp.mean(wide**2, -1, keepdims=True) + 1e-6)
    return (wide * scale).astype(jnp.bfloat16)


def layer(h, w):
    a = normed(h)
    gate = jnp.dot(a, w["w_gate"], preferred_element_type=jnp.float32)
    up = jnp.dot(a, w["w_up"], preferred_element_type=jnp.float32)
    return h + matmul((jax.nn.silu(gate) * up).astype(jnp.bfloat16), w["w_down"])


def stage(weights, h):
    for number in range(weights["w_gate"].shape[0]):
        h = layer(h, {name: w[number] for name, w in weights.items()})
    return h


def solution(mesh):
    stages = mesh.shape["pp"]
    onward = [(i, i + 1) for i in range(stages - 1)]
    back_again = [(i + 1, i) for i in range(stages - 1)]

    def step(x, dy, *arrays):
        weights = dict(zip(NAMES, arrays, strict=True))
        micro, me = x.shape[0], lax.axis_index("pp")
        kept, came = jnp.zeros_like(x), jnp.zeros_like(x[0])
        for t in range(micro + stages - 1):
            number = jnp.clip(t - me, 0, micro - 1)
            at_work = (t >= me) & (t - me < micro)
            h = jnp.where(me == 0, x[min(t, micro - 1)], came)
            was = lax.dynamic_index_in_dim(kept, number, 0, keepdims=False)
            kept = lax.dynamic_update_index_in_dim(kept, jnp.where(at_work, h, was), number, 0)
            came = lax.ppermute(stage(weights, h), "pp", onward)
        total = {name: jnp.zeros(w.shape, jnp.float32) for name, w in weights.items()}
        came, behind = jnp.zeros_like(x[0]), stages - 1 - me
        for t in range(micro + stages - 1):
            number = jnp.clip(t - behind, 0, micro - 1)
            at_work = (t >= behind) & (t - behind < micro)
            by_y = jnp.where(behind == 0, dy[min(t, micro - 1)], came)
            _, back = jax.vjp(stage, weights, lax.dynamic_index_in_dim(kept, number, 0, keepdims=False))
            by_w, by_h = back(by_y)
            total = {name: total[name] + jnp.where(at_work, by_w[name].astype(jnp.float32), 0.0) for name in NAMES}
            came = lax.ppermute(by_h, "pp", back_again)
        return tuple(total[name].astype(jnp.bfloat16) for name in NAMES)

    return jax.shard_map(
        step,
        mesh=mesh,
        in_specs=(P("rep", None, None),) * 2 + (P("pp", None, None),) * 3,
        out_specs=(P(("rep", "pp"), None, None),) * 3,
        check_vma=False,
    )
```

profile of v0, /device:TPU:19, one launch (start us, length us, event | category | flops | bytes accessed | tf_op | source)
XLA Modules:
  0.0 1142.8 jit_solution(958636068942598906)
XLA Ops:
  15.1 6.1 collective-permute-done
  26.0 5.7 fusion.831
  36.1 6.1 collective-permute-done.1
  47.0 5.7 fusion.828
  57.1 6.1 collective-permute-done.2
  68.0 5.7 fusion.825
  78.3 5.9 collective-permute-done.3
  89.0 5.7 fusion.822
  99.2 6.1 collective-permute-done.4
  110.1 5.7 fusion.819
  120.2 6.1 collective-permute-done.5
  131.1 5.7 fusion.816
  141.2 6.1 collective-permute-done.6
  152.1 5.7 fusion.813
  162.5 5.9 collective-permute-done.7
  173.1 5.7 fusion.810
  183.3 6.1 collective-permute-done.8
  194.2 5.7 fusion.807
  204.4 6.0 collective-permute-done.9
  215.4 5.3 fusion.804
  257.7 5.3 fusion.798
  320.7 5.3 fusion.789
  341.5 5.4 fusion.786
  362.1 5.4 fusion.783
  382.8 5.4 fusion.780
  403.5 5.4 fusion.777
  424.6 5.4 fusion.774
  444.9 5.4 fusion.771
  477.5 6.1 fusion.1007
  1089.0 17.4 %fusion.102 = bf16[1,512,1536]{2,1,0:T(8,128)(2,1)} fusion(bf16[512,1536]{1,0:T(8,128)(2,1)} %copy-done.105, bf16[512,1536]{1,0:T(8,128)(2,1)} %convolution_convert_fusion.46, bf16[512,1536]{1,0:T(8,128)(2,1)} %convolution_convert_fusion.47, bf16[512,1536]{1,0:T(8,128)(2,1)} %convolution_convert_fusion.48, ...), kind=kOutput, calls=%fused_computation.329 | convolution fusion | flops 865861632 | bytes 41420828 | tf_op jit(solution)/shard_map/transpose(jvp())/dot_general | solution.py:22
  1106.4 18.2 %fusion.101 = bf16[1,512,1536]{2,1,0:T(8,128)(2,1)} fusion(bf16[512,1536]{1,0:T(8,128)(2,1)} %fusion.74, bf16[512,1536]{1,0:T(8,128)(2,1)S(1)} %copy-done.108, bf16[512,1536]{1,0:T(8,128)(2,1)} %convolution_convert_fusion.69, bf16[512,1536]{1,0:T(8,128)(2,1)} %convolution_convert_fusion.70, bf16[512,1536]{1,0:T(8,128)(2,1)} %convolution_convert_fusion.71, ...), kind=kOutput, calls=%fused_computation.328 | convolution fusion | flops 860356608 | bytes 38275100 | tf_op jit(solution)/shard_map/transpose(jvp())/dot_general | solution.py:21
  1124.6 17.9 %fusion.100 = bf16[1,1536,512]{2,1,0:T(8,128)(2,1)} fusion(bf16[1536,512]{1,0:T(8,128)(2,1)} %convolution_convert_fusion.1, bf16[1536,512]{1,0:T(8,128)(2,1)} %convolution_convert_fusion.2, bf16[1536,512]{1,0:T(8,128)(2,1)} %convolution_convert_fusion.3, bf16[1536,512]{1,0:T(8,128)(2,1)} %convolution_convert_fusion.4, ...), kind=kOutput, calls=%fused_computation.327 | convolution fusion | flops 865337344 | bytes 43515928 | tf_op jit(solution)/shard_map/transpose(jvp())/dot_general | solution.py:10
  (684 shorter events, 919.2 us)
Async XLA Ops:
  52.7 10.5 collective-permute-start.2
  94.8 10.5 collective-permute-start.4
  115.8 10.5 collective-permute-start.5
  200.0 10.5 collective-permute-start.9
  220.7 13.8 %collective-permute-start.10 = (bf16[512,512]{1,0:T(8,128)(2,1)}, bf16[512,512]{1,0:T(8,128)(2,1)S(1)}, u32[]{:S(2)}, u32[]{:S(2)}) collective-permute-start(bf16[512,512]{1,0:T(8,128)(2,1)} %fusion.804), channel_id=1, source_target_pairs={{0,1},{1,2},{2,3},{3,4},{4,5},{5,6},{6,7},{8,9},{9,10},{10,11},{11... | collective-permute-start | bytes 1572872 | tf_op jit(solution)/shard_map/ppermute | solution.py:47
  263.0 10.5 collective-permute-start.12
  283.7 11.3 collective-permute-start.13
  305.2 10.6 collective-permute-start.14
  326.0 10.7 collective-permute-start.15
  408.9 10.9 collective-permute-start.19
  485.6 67.4 %collective-permute-start.22 = (bf16[512,512]{1,0:T(8,128)(2,1)S(1)}, bf16[512,512]{1,0:T(8,128)(2,1)S(1)}, u32[]{:S(2)}, u32[]{:S(2)}) collective-permute-start(bf16[512,512]{1,0:T(8,128)(2,1)S(1)} %fusion.1105), channel_id=1, source_target_pairs={{1,0},{2,1},{3,2},{4,3},{5,4},{6,5},{7,6},{9,8},{10,9},{11,10},{12... | collective-permute-start | bytes 1572872 | tf_op jit(solution)/shard_map/ppermute | solution.py:57
  568.5 14.4 %collective-permute-start.23 = (bf16[512,512]{1,0:T(8,128)(2,1)S(1)}, bf16[512,512]{1,0:T(8,128)(2,1)S(1)}, u32[]{:S(2)}, u32[]{:S(2)}) collective-permute-start(bf16[512,512]{1,0:T(8,128)(2,1)S(1)} %fusion.1104), channel_id=1, source_target_pairs={{1,0},{2,1},{3,2},{4,3},{5,4},{6,5},{7,6},{9,8},{10,9},{11,10},{12... | collective-permute-start | bytes 1572872 | tf_op jit(solution)/shard_map/ppermute | solution.py:57
  597.3 10.5 collective-permute-start.24
  622.3 10.5 collective-permute-start.25
  647.3 10.5 collective-permute-start.26
  672.2 10.5 collective-permute-start.27
  697.1 10.5 collective-permute-start.28
  722.1 10.5 collective-permute-start.29
  747.0 10.5 collective-permute-start.30
  771.9 10.5 collective-permute-start.31
  796.8 10.5 collective-permute-start.32
  821.7 10.5 collective-permute-start.33
  846.6 10.5 collective-permute-start.34
  871.5 10.5 collective-permute-start.35
  896.4 10.5 collective-permute-start.36
  921.3 10.5 collective-permute-start.37
  946.3 10.5 collective-permute-start.38
  971.2 10.5 collective-permute-start.39
  996.1 10.5 collective-permute-start.40
  1021.0 10.5 collective-permute-start.41
  1046.1 10.5 collective-permute-start.42
  1072.2 10.5 collective-permute-start.43
  (123 other events, 1090.5 us)
where the time goes:
time: 1160 us; the launch traced here: 1140 us
  matrix products  685 us (59%)
  waiting for transfers between devices  157 us (14%)
  starting transfers between devices  136 us (12%)
  other arithmetic  107 us (9%)
  local copies, waits for them, and re-layouts  53.9 us (5%)
    dot_general x90, matrix products, layer(): gate = jnp.dot(a, w['w_gate'], preferred_element_type=jnp.float32)  241 us
    dot_general x68, matrix products, layer(): up = jnp.dot(a, w['w_up'], preferred_element_type=jnp.float32)  227 us
    dot_general x68, matrix products, matmul(): jnp.dot(a, w, preferred_element_type=jnp.float32).astype(jnp.bfloat16)  216 us
    ppermute x22, waiting for transfers between devices, step(): came = lax.ppermute(by_h, 'pp', back_again)  94.2 us
    ppermute x22, starting transfers between devices, step(): came = lax.ppermute(stage(weights, h), 'pp', onward)  86.8 us
    ppermute x22, waiting for transfers between devices, step(): came = lax.ppermute(stage(weights, h), 'pp', onward)  62.9 us
    ppermute x22, starting transfers between devices, step(): came = lax.ppermute(by_h, 'pp', back_again)  49.4 us
    dynamic_update_slice x23, other arithmetic, step(): lax.dynamic_update_index_in_dim(kept, jnp.where(at_work, h, was), number, 0)  44 us
  transfers between devices with their start and end apart: 44, of which 33 were waited for; matrix products, arithmetic and copies ran while one was open for 20% of the time, Pallas kernels for 0%

commit v1 on v0

v1 whole, which is shorter than its diff:
```python
import functools

import jax
import jax.numpy as jnp
from jax import lax
from jax.experimental import pallas as pl
from jax.experimental.pallas import tpu as pltpu
from jax.sharding import PartitionSpec as P

F32, BF16 = jnp.float32, jnp.bfloat16
CUTS = 4
TILE = 512


def dot(a, b):
    return jnp.dot(a, b, preferred_element_type=F32)


def rounded(x):
    return x.astype(BF16).astype(F32)


def scale_of(wide):
    return lax.rsqrt(jnp.mean(wide * wide, -1, keepdims=True) + 1e-6)


def sigmoid(x):
    return 1.0 / (1.0 + jnp.exp(-x))


def kernel(stages, x, dy, w_gate, w_up, w_down, out_gate, out_up, out_down, gu_far,
           wg, wu, wd, wgt, wut, wdt, ahead, behind, send_a, send_b, gu, hid, dgate, dup, at, dyt, tot_g, tot_u, tot_d,
           a_blk, h_blk, sem_w, sem_a, sem_b, sem_sa, sem_sb, sem_far, sem_near, sem_out):
    micro, tokens, width = ahead.shape
    ff = wg.shape[1]
    rows_n = tokens // CUTS
    me = lax.axis_index("pp")
    last = stages - 1
    first_stage, last_stage = me == 0, me == last
    to_go = last - me
    delay = 1 + to_go + to_go // 2

    def rows(c):
        return pl.ds(c * rows_n, rows_n)

    def take_x(k, c):
        return pltpu.make_async_copy(x.at[k, rows(c)], ahead.at[k, rows(c)], sem_a.at[k, c])

    def take_dy(k, c):
        return pltpu.make_async_copy(dy.at[k, rows(c)], behind.at[k, rows(c)], sem_b.at[k, c])

    loads = [pltpu.make_async_copy(src.at[0], dst, sem_w.at[i]) for i, (src, dst) in enumerate(((w_gate, wg), (w_up, wu), (w_down, wd)))]

    @pl.when(first_stage)
    def _():
        for c in range(CUTS):
            take_x(0, c).start()

    for load in loads:
        load.start()

    @pl.when(first_stage)
    def _():
        @pl.loop(1, micro)
        def _(k):
            for c in range(CUTS):
                take_x(k, c).start()

    @pl.when(last_stage)
    def _():
        @pl.loop(0, micro)
        def _(k):
            for c in range(CUTS):
                take_dy(k, c).start()

    barrier = pltpu.get_barrier_semaphore()

    @pl.when(me > 0)
    def _():
        pl.semaphore_signal(barrier, inc=1, device_id={"pp": me - 1}, device_id_type=pl.DeviceIdType.MESH)

    @pl.when(me < last)
    def _():
        pl.semaphore_signal(barrier, inc=1, device_id={"pp": me + 1}, device_id_type=pl.DeviceIdType.MESH)

    pl.semaphore_wait(barrier, jnp.minimum(me, 1) + jnp.minimum(last - me, 1))

    def pass_on(k, c):
        return pltpu.make_async_remote_copy(
            src_ref=send_a.at[k % 2, rows(c)], dst_ref=ahead.at[k, rows(c)], send_sem=sem_sa.at[k % 2, c], recv_sem=sem_a.at[k, c],
            device_id={"pp": jnp.minimum(me + 1, last)}, device_id_type=pl.DeviceIdType.MESH)

    def pass_back(m, c):
        return pltpu.make_async_remote_copy(
            src_ref=send_b.at[m % 2, rows(c)], dst_ref=behind.at[m, rows(c)], send_sem=sem_sb.at[m % 2, c], recv_sem=sem_b.at[m, c],
            device_id={"pp": jnp.maximum(me - 1, 0)}, device_id_type=pl.DeviceIdType.MESH)

    def put_away(k, c):
        return pltpu.make_async_copy(gu.at[c], gu_far.at[k, c], sem_far.at[c])

    def fetch(m, c):
        return pltpu.make_async_copy(gu_far.at[m, c], gu.at[CUTS + c], sem_near.at[c])

    def forward(k):
        for c in range(CUTS):
            take_x(k, c).wait()

            @pl.when((me < last) & (k >= 1))
            def _():
                put_away(k - 1, c).wait()

            wide = ahead[k, rows(c), :].astype(F32)
            a_blk[...] = (wide * scale_of(wide)).astype(BF16)
            for n in range(0, ff, TILE):
                g = dot(a_blk[...], wg[:, n:n + TILE])
                u = dot(a_blk[...], wu[:, n:n + TILE])
                gu[c, :, n:n + TILE] = g
                gu[c, :, ff + n:ff + n + TILE] = u
                h_blk[:, n:n + TILE] = (g * sigmoid(g) * u).astype(BF16)

            @pl.when(me < last)
            def _():
                put_away(k, c).start()

                @pl.when(k >= 2)
                def _():
                    pass_on(k, c).wait_send()

                y = rounded(dot(h_blk[...], wd[...]))
                send_a[k % 2, rows(c), :] = (ahead[k, rows(c), :].astype(F32) + y).astype(BF16)
                pass_on(k, c).start()

    def backward(m):
        base = jnp.where(me < last, CUTS, 0)
        for c in range(CUTS):
            take_dy(m, c).wait()

            @pl.when(me < last)
            def _():
                fetch(m, c).wait()

            for n in range(0, ff, TILE):
                dh = rounded(dot(behind[m, rows(c), :], wdt[:, n:n + TILE]))
                g = gu[base + c, :, n:n + TILE]
                u = gu[base + c, :, ff + n:ff + n + TILE]
                s = sigmoid(g)
                t = g * s
                hid[rows(c), n:n + TILE] = (t * u).astype(BF16)
                dup[rows(c), n:n + TILE] = (dh * t).astype(BF16)
                dgate[rows(c), n:n + TILE] = (dh * u * (s + t * (1.0 - s))).astype(BF16)

            @pl.when(me > 0)
            def _():
                @pl.when(m >= 2)
                def _():
                    pass_back(m, c).wait_send()

                da = rounded(dot(dup[rows(c), :], wut[...])) + rounded(dot(dgate[rows(c), :], wgt[...]))
                da = rounded(da)
                wide = ahead[m, rows(c), :].astype(F32)
                scale = scale_of(wide)
                inner = jnp.sum(da * wide, -1, keepdims=True)
                by_norm = rounded(da * scale + (inner * (scale * scale * scale) * (-1.0 / width)) * wide)
                send_b[m % 2, rows(c), :] = (behind[m, rows(c), :].astype(F32) + by_norm).astype(BF16)
                pass_back(m, c).start()

    def weights(m):
        wide = ahead[m].astype(F32)
        at[...] = (wide * scale_of(wide)).astype(BF16).T
        dyt[...] = behind[m].T
        for n in range(0, ff, TILE):
            tot_g[:, n:n + TILE] += rounded(dot(at[...], dgate[:, n:n + TILE]))
            tot_u[:, n:n + TILE] += rounded(dot(at[...], dup[:, n:n + TILE]))
            tot_d[:, n:n + TILE] += rounded(dot(dyt[...], hid[:, n:n + TILE]))

    for load in loads:
        load.wait()

    @pl.loop(0, micro + delay)
    def _(k):
        m = k - delay

        @pl.when(m >= 0)
        def _():
            backward(m)

        @pl.when(k < micro)
        def _():
            forward(k)

        @pl.when((me < last) & (k == micro))
        def _():
            for c in range(CUTS):
                put_away(micro - 1, c).wait()

        @pl.when((me < last) & (m + 1 >= 0) & (m + 1 < micro))
        def _():
            for c in range(CUTS):
                fetch(m + 1, c).start()

        @pl.when(k == 0)
        def _():
            wdt[...] = wd[...].T
            wgt[...] = wg[...].T
            wut[...] = wu[...].T
            tot_g[...] = jnp.zeros_like(tot_g)
            tot_u[...] = jnp.zeros_like(tot_u)
            tot_d[...] = jnp.zeros_like(tot_d)

        @pl.when(m >= 0)
        def _():
            weights(m)

    dgate[...] = tot_g[...].astype(BF16)
    dup[...] = tot_u[...].astype(BF16)
    hid[...] = tot_d[...].astype(BF16)
    stores = [pltpu.make_async_copy(src, dst.at[0], sem_out.at[i])
              for i, (src, dst) in enumerate(((dgate, out_gate), (dup, out_up), (hid, out_down)))]
    for store in stores:
        store.start()

    @pl.when(me < last)
    def _():
        for k in (micro - 2, micro - 1):
            for c in range(CUTS):
                pass_on(k, c).wait_send()

    @pl.when(me > 0)
    def _():
        for m in (micro - 2, micro - 1):
            for c in range(CUTS):
                pass_back(m, c).wait_send()

    for store in stores:
        store.wait()


def solution(mesh):
    stages = mesh.shape["pp"]

    def step(x, dy, w_gate, w_up, w_down):
        micro, tokens, width = x.shape
        ff = w_gate.shape[2]
        whole = (micro, tokens, width)
        rows_n = tokens // CUTS
        vmem, dma = pltpu.VMEM, pltpu.SemaphoreType.DMA
        any_space = pl.BlockSpec(memory_space=pl.ANY)
        g, u, d, _ = pl.pallas_call(
            functools.partial(kernel, stages),
            out_shape=(jax.ShapeDtypeStruct((1, width, ff), BF16),) * 3
            + (jax.ShapeDtypeStruct((micro, CUTS, rows_n, 2 * ff), F32),),
            in_specs=[any_space] * 5,
            out_specs=(any_space,) * 4,
            scratch_shapes=[
                vmem((width, ff), BF16), vmem((width, ff), BF16), vmem((ff, width), BF16),
                vmem((ff, width), BF16), vmem((ff, width), BF16), vmem((width, ff), BF16),
                vmem(whole, BF16), vmem(whole, BF16),
                vmem((2, tokens, width), BF16), vmem((2, tokens, width), BF16),
                vmem((2 * CUTS, rows_n, 2 * ff), F32),
                vmem((tokens, ff), BF16), vmem((tokens, ff), BF16), vmem((tokens, ff), BF16),
                vmem((width, tokens), BF16), vmem((width, tokens), BF16),
                vmem((width, ff), F32), vmem((width, ff), F32), vmem((width, ff), F32),
                vmem((rows_n, width), BF16), vmem((rows_n, ff), BF16),
                dma((3,)), dma((micro, CUTS)), dma((micro, CUTS)), dma((2, CUTS)), dma((2, CUTS)),
                dma((CUTS,)), dma((CUTS,)), dma((3,)),
            ],
            compiler_params=pltpu.CompilerParams(collective_id=0, has_side_effects=True, vmem_limit_bytes=67_000_000),
            name="pipeline",
        )(x, dy, w_gate, w_up, w_down)
        return g, u, d.transpose(0, 2, 1)

    return jax.shard_map(
        step,
        mesh=mesh,
        in_specs=(P("rep", None, None),) * 2 + (P("pp", None, None),) * 3,
        out_specs=(P(("rep", "pp"), None, None),) * 3,
        check_vma=False,
    )
```

time: 1160 us -> 256 us (0.22)
  the two profiles are of different devices: /device:TPU:19 before, /device:TPU:2 now
where the time goes in v1:
time: 256 us
  Pallas kernels  249 us (97%)
  local copies, waits for them, and re-layouts  5.83 us (2%)
    pallas_call x1, Pallas kernels, step(): pl.pallas_call(functools.partial(kernel, stages), out_shape=(jax.ShapeDty...  249 us
    unnamed x7, local copies, waits for them, and re-layouts  5.83 us

profile of v1, /device:TPU:2, one launch (start us, length us, event | category | flops | bytes accessed | tf_op | source)
XLA Modules:
  0.0 256.0 jit_solution(5530185998299203378)
XLA Ops:
  0.6 249.5 %pipeline.1 = (bf16[1,512,1536]{2,1,0:T(8,128)(2,1)}, bf16[1,512,1536]{2,1,0:T(8,128)(2,1)}, bf16[1,512,1536]{2,1,0:T(8,128)(2,1)}, f32[16,4,128,3072]{3,2,1,0:T(8,128)}) custom-call(bf16[16,512,512]{2,1,0:T(8,128)(2,1)} %x.1, bf16[16,512,512]{2,1,0:T(8,128)(2,1)} %dy.1, bf16[1,512,1536]{2,1,0:T(8,128)(2,1)} %w_gate.1, bf16[1,512,1536]{2,1,0:T(8,128)(2,1)} %w_up.1, ...), custom_call_target="tpu_custom_call" | custom-call | tf_op jit(solution)/shard_map/pipeline/pallas_call | solution.py:248
  250.1 0.0 copy-start.1
  250.1 2.7 %copy.8 = bf16[1,1536,512]{2,1,0:T(8,128)(2,1)} copy(bf16[1,1536,512]{1,2,0:T(8,128)(2,1)} %bitcast.1) | data formatting | bytes 3145728
  252.8 0.0 copy-done.1
  252.8 0.0 copy-start
  252.8 1.1 copy.11
  254.0 0.8 copy-done
  254.8 1.1 copy.12
Async XLA Ops:
  250.1 2.7 %copy-start.1 = (bf16[1,512,1536]{2,1,0:T(8,128)(2,1)S(1)}, bf16[1,512,1536]{2,1,0:T(8,128)(2,1)}, u32[]{:S(2)}) copy-start(bf16[1,512,1536]{2,1,0:T(8,128)(2,1)} %get-tuple-element.15) | copy-start | bytes 4718596
  252.8 2.0 copy-start

commit v2 on v0

v2 whole, which is shorter than its diff:
```python
import jax
import jax.numpy as jnp
from jax import lax
from jax.experimental import pallas as pl
from jax.experimental.pallas import tpu as pltpu
from jax.sharding import PartitionSpec as P

F32, BF16 = jnp.float32, jnp.bfloat16
CUTS = 4
TILE = 512


def dot(a, b):
    return jnp.dot(a, b, preferred_element_type=F32)


def rounded(x):
    return x.astype(BF16).astype(F32)


def scale_of(wide):
    return lax.rsqrt(jnp.mean(wide * wide, -1, keepdims=True) + 1e-6)


def kernel(x, dy, w_gate, w_up, w_down, out_gate, out_up, out_down, far_act, far_hid,
           wg, wu, wd, wgt, wut, wdt, ahead, behind, send_a, send_b, act, hidden, dgate, dup, at, dyt, tot_g, tot_u, tot_d,
           a_blk, sem_w, sem_a, sem_b, sem_sa, sem_sb, sem_far, sem_near, sem_hfar, sem_hnear, sem_out):
    micro, tokens, width = ahead.shape
    ff = wg.shape[1]
    rows_n = tokens // CUTS
    me, last = lax.axis_index("pp"), lax.axis_size("pp") - 1
    to_go = last - me
    delay = to_go + to_go // 2
    near = delay == 1

    def rows(c):
        return pl.ds(pl.multiple_of(c * rows_n, rows_n), rows_n)

    def each(f):
        pl.loop(0, CUTS)(f)

    def take_x(k, c):
        return pltpu.make_async_copy(x.at[k, rows(c)], ahead.at[k, rows(c)], sem_a.at[k, c])

    def take_dy(k, c):
        return pltpu.make_async_copy(dy.at[k, rows(c)], behind.at[k, rows(c)], sem_b.at[k, c])

    loads = [pltpu.make_async_copy(src.at[0], dst, sem_w.at[i]) for i, (src, dst) in enumerate(((w_gate, wg), (w_up, wu), (w_down, wd)))]

    @pl.when(me == 0)
    def _():
        each(lambda c: take_x(0, c).start())

    for load in loads:
        load.start()

    @pl.when(me == 0)
    def _():
        @pl.loop(1, micro)
        def _(k):
            each(lambda c: take_x(k, c).start())

    @pl.when(me == last)
    def _():
        @pl.loop(0, micro)
        def _(k):
            each(lambda c: take_dy(k, c).start())

    barrier = pltpu.get_barrier_semaphore()

    @pl.when(me > 0)
    def _():
        pl.semaphore_signal(barrier, inc=1, device_id={"pp": me - 1}, device_id_type=pl.DeviceIdType.MESH)

    @pl.when(me < last)
    def _():
        pl.semaphore_signal(barrier, inc=1, device_id={"pp": me + 1}, device_id_type=pl.DeviceIdType.MESH)

    pl.semaphore_wait(barrier, jnp.minimum(me, 1) + jnp.minimum(last - me, 1))

    def pass_on(k, c):
        return pltpu.make_async_remote_copy(
            src_ref=send_a.at[k % 2, rows(c)], dst_ref=ahead.at[k, rows(c)], send_sem=sem_sa.at[k % 2, c], recv_sem=sem_a.at[k, c],
            device_id={"pp": jnp.minimum(me + 1, last)}, device_id_type=pl.DeviceIdType.MESH)

    def pass_back(m, c):
        return pltpu.make_async_remote_copy(
            src_ref=send_b.at[m % 2, rows(c)], dst_ref=behind.at[m, rows(c)], send_sem=sem_sb.at[m % 2, c], recv_sem=sem_b.at[m, c],
            device_id={"pp": jnp.maximum(me - 1, 0)}, device_id_type=pl.DeviceIdType.MESH)

    def slot_f(k):
        return jnp.where(near, k % 2, 0)

    def slot_b(m):
        return jnp.where(near, m % 2, 1)

    def put_away(k, c):
        return (pltpu.make_async_copy(act.at[0, c], far_act.at[k, c], sem_far.at[c]),
                pltpu.make_async_copy(hidden.at[0, rows(c)], far_hid.at[k, rows(c)], sem_hfar.at[c]))

    def fetch(m, c):
        return pltpu.make_async_copy(far_act.at[m, c], act.at[1, c], sem_near.at[c])

    def fetch_hidden(m):
        return pltpu.make_async_copy(far_hid.at[m], hidden.at[1], sem_hnear.at[0])

    def silu_parts(g, u):
        half = 0.5 * g
        z = jnp.tanh(half)
        q = half * z
        return half + q, u * ((0.5 * z + 0.5) * ((half - q) + 1.0))

    def work_forward(k, c):
        slot = slot_f(k)
        wide = ahead[k, rows(c), :].astype(F32)
        a_blk[...] = (wide * scale_of(wide)).astype(BF16)
        for n in range(0, ff, TILE):
            g = dot(a_blk[...], wg[:, n:n + TILE])
            u = dot(a_blk[...], wu[:, n:n + TILE])
            t, v = silu_parts(g, u)
            act[slot, c, :, n:n + TILE] = t
            act[slot, c, :, ff + n:ff + n + TILE] = v
            hidden[slot, rows(c), n:n + TILE] = (t * u).astype(BF16)
        y = rounded(dot(hidden[slot, rows(c), :], wd[...]))
        send_a[k % 2, rows(c), :] = (ahead[k, rows(c), :].astype(F32) + y).astype(BF16)

    def by_hidden(m, c):
        slot = slot_b(m)
        for n in range(0, ff, TILE):
            dh = rounded(dot(behind[m, rows(c), :], wdt[:, n:n + TILE]))
            dup[rows(c), n:n + TILE] = (dh * act[slot, c, :, n:n + TILE]).astype(BF16)
            dgate[rows(c), n:n + TILE] = (dh * act[slot, c, :, ff + n:ff + n + TILE]).astype(BF16)

    def by_input(m, c):
        da = rounded(rounded(dot(dup[rows(c), :], wut[...])) + rounded(dot(dgate[rows(c), :], wgt[...])))
        wide = ahead[m, rows(c), :].astype(F32)
        scale = scale_of(wide)
        inner = jnp.sum(da * wide, -1, keepdims=True)
        by_norm = rounded(da * scale + (inner * (scale * scale * scale) * (-1.0 / width)) * wide)
        send_b[m % 2, rows(c), :] = (behind[m, rows(c), :].astype(F32) + by_norm).astype(BF16)

    def work_last(k, c):
        wide = ahead[k, rows(c), :].astype(F32)
        a_blk[...] = (wide * scale_of(wide)).astype(BF16)
        for n in range(0, ff, TILE):
            g = dot(a_blk[...], wg[:, n:n + TILE])
            u = dot(a_blk[...], wu[:, n:n + TILE])
            dh = rounded(dot(behind[k, rows(c), :], wdt[:, n:n + TILE]))
            t, v = silu_parts(g, u)
            hidden[0, rows(c), n:n + TILE] = (t * u).astype(BF16)
            dup[rows(c), n:n + TILE] = (dh * t).astype(BF16)
            dgate[rows(c), n:n + TILE] = (dh * v).astype(BF16)
        by_input(k, c)

    def weights(m, slot):
        wide = ahead[m].astype(F32)
        at[...] = (wide * scale_of(wide)).astype(BF16).T
        dyt[...] = behind[m].T
        for n in range(0, ff, TILE):
            tot_g[:, n:n + TILE] += rounded(dot(at[...], dgate[:, n:n + TILE]))
            tot_u[:, n:n + TILE] += rounded(dot(at[...], dup[:, n:n + TILE]))
            tot_d[:, n:n + TILE] += rounded(dot(dyt[...], hidden[slot, :, n:n + TILE]))

    def before_forward(k, c):
        take_x(k, c).wait()

        @pl.when((k >= 1) & ~near)
        def _():
            for copy in put_away(k - 1, c):
                copy.wait()

        @pl.when(k >= 2)
        def _():
            pass_on(k, c).wait_send()

    def after_forward(k, c):
        pass_on(k, c).start()

        @pl.when(~near)
        def _():
            for copy in put_away(k, c):
                copy.start()

    def before_backward(m, c, send):
        take_dy(m, c).wait()

        @pl.when(~near)
        def _():
            fetch(m, c).wait()

        if send:
            @pl.when(m >= 2)
            def _():
                pass_back(m, c).wait_send()

    def turn():
        wdt[...] = wd[...].T
        wgt[...] = wg[...].T
        wut[...] = wu[...].T

    def clear():
        tot_g[...] = jnp.zeros_like(tot_g)
        tot_u[...] = jnp.zeros_like(tot_u)
        tot_d[...] = jnp.zeros_like(tot_d)

    def run(send):
        @pl.loop(0, micro + delay)
        def _(k):
            m = k - delay

            @pl.when(m < 0)
            def _():
                @each
                def _(c):
                    before_forward(k, c)
                    work_forward(k, c)
                    after_forward(k, c)

            @pl.when((m >= 0) & (k < micro))
            def _():
                @each
                def _(c):
                    before_backward(m, c, send)
                    before_forward(k, c)
                    work_forward(k, c)
                    by_hidden(m, c)
                    if send:
                        by_input(m, c)
                        pass_back(m, c).start()
                    after_forward(k, c)

            @pl.when(k >= micro)
            def _():
                @each
                def _(c):
                    before_backward(m, c, send)
                    by_hidden(m, c)
                    if send:
                        by_input(m, c)
                        pass_back(m, c).start()

            @pl.when((k == micro) & ~near)
            def _():
                @each
                def _(c):
                    for copy in put_away(micro - 1, c):
                        copy.wait()

            coming = (m + 1 >= 0) & (m + 1 < micro) & ~near

            @pl.when(coming)
            def _():
                each(lambda c: fetch(m + 1, c).start())

            @pl.when(k == 0)
            def _():
                turn()
                clear()

            @pl.when(m >= 0)
            def _():
                @pl.when(~near)
                def _():
                    fetch_hidden(m).wait()

                weights(m, slot_b(m))

            @pl.when(coming)
            def _():
                fetch_hidden(m + 1).start()

    for load in loads:
        load.wait()

    @pl.when(me == 0)
    def _():
        run(False)

    @pl.when((me > 0) & (me < last))
    def _():
        run(True)

    @pl.when(me == last)
    def _():
        turn()
        clear()

        @pl.loop(0, micro)
        def _(k):
            @each
            def _(c):
                take_x(k, c).wait()
                take_dy(k, c).wait()

                @pl.when(k >= 2)
                def _():
                    pass_back(k, c).wait_send()

                work_last(k, c)
                pass_back(k, c).start()

            weights(k, 0)

    dgate[...] = tot_g[...].astype(BF16)
    stores = [pltpu.make_async_copy(src, dst.at[0], sem_out.at[i])
              for i, (src, dst) in enumerate(((dgate, out_gate), (dup, out_up), (wd, out_down)))]
    stores[0].start()
    dup[...] = tot_u[...].astype(BF16)
    stores[1].start()
    wd[...] = tot_d[...].astype(BF16).T
    stores[2].start()

    @pl.when(me < last)
    def _():
        for k in (micro - 2, micro - 1):
            each(lambda c, k=k: pass_on(k, c).wait_send())

    @pl.when(me > 0)
    def _():
        for m in (micro - 2, micro - 1):
            each(lambda c, m=m: pass_back(m, c).wait_send())

    for store in stores:
        store.wait()


def solution(mesh):
    def step(x, dy, w_gate, w_up, w_down):
        micro, tokens, width = x.shape
        ff = w_gate.shape[2]
        rows_n = tokens // CUTS
        vmem, dma = pltpu.VMEM, pltpu.SemaphoreType.DMA
        any_space = pl.BlockSpec(memory_space=pl.ANY)
        g, u, d, _, _ = pl.pallas_call(
            kernel,
            out_shape=(
                jax.ShapeDtypeStruct((1, width, ff), BF16), jax.ShapeDtypeStruct((1, width, ff), BF16),
                jax.ShapeDtypeStruct((1, ff, width), BF16),
                jax.ShapeDtypeStruct((micro, CUTS, rows_n, 2 * ff), F32), jax.ShapeDtypeStruct((micro, tokens, ff), BF16)),
            in_specs=[any_space] * 5,
            out_specs=(any_space,) * 5,
            scratch_shapes=[
                vmem((width, ff), BF16), vmem((width, ff), BF16), vmem((ff, width), BF16),
                vmem((ff, width), BF16), vmem((ff, width), BF16), vmem((width, ff), BF16),
                vmem(x.shape, BF16), vmem(x.shape, BF16),
                vmem((2, tokens, width), BF16), vmem((2, tokens, width), BF16),
                vmem((2, CUTS, rows_n, 2 * ff), F32), vmem((2, tokens, ff), BF16),
                vmem((tokens, ff), BF16), vmem((tokens, ff), BF16),
                vmem((width, tokens), BF16), vmem((width, tokens), BF16),
                vmem((width, ff), F32), vmem((width, ff), F32), vmem((width, ff), F32),
                vmem((rows_n, width), BF16),
                dma((3,)), dma((micro, CUTS)), dma((micro, CUTS)), dma((2, CUTS)), dma((2, CUTS)),
                dma((CUTS,)), dma((CUTS,)), dma((CUTS,)), dma((1,)), dma((3,)),
            ],
            compiler_params=pltpu.CompilerParams(collective_id=0, has_side_effects=True, vmem_limit_bytes=67_000_000),
            name="pipeline",
        )(x, dy, w_gate, w_up, w_down)
        return g, u, d

    return jax.shard_map(
        step,
        mesh=mesh,
        in_specs=(P("rep", None, None),) * 2 + (P("pp", None, None),) * 3,
        out_specs=(P(("rep", "pp"), None, None),) * 3,
        check_vma=False,
    )
```

time: 1160 us -> 216 us (0.19)
  the two profiles are of different devices: /device:TPU:19 before, /device:TPU:2 now
where the time goes in v2:
time: 216 us
  Pallas kernels  209 us (97%)
  local copies, waits for them, and re-layouts  5.89 us (3%)
    pallas_call x1, Pallas kernels, step(): pl.pallas_call(kernel, out_shape=(jax.ShapeDtypeStruct((1, width, ff), BF...  209 us
    unnamed x7, local copies, waits for them, and re-layouts  5.89 us

profile of v2, /device:TPU:2, one launch (start us, length us, event | category | flops | bytes accessed | tf_op | source)
XLA Modules:
  0.0 215.6 jit_solution(18136015517523677687)
XLA Ops:
  0.6 209.1 %pipeline.1 = (bf16[1,512,1536]{2,1,0:T(8,128)(2,1)}, bf16[1,512,1536]{2,1,0:T(8,128)(2,1)}, bf16[1,1536,512]{2,1,0:T(8,128)(2,1)}, f32[16,4,128,3072]{3,2,1,0:T(8,128)}, bf16[16,512,1536]{2,1,0:T(8,128)(2,1)}) custom-call(bf16[16,512,512]{2,1,0:T(8,128)(2,1)} %x.1, bf16[16,512,512]{2,1,0:T(8,128)(2,1)} %dy.1, bf16[1,512,1536]{2,1,0:T(8,128)(2,1)} %w_gate.1, ...), custom_call_target="tpu_custom_call" | custom-call | tf_op jit(solution)/shard_map/pipeline/pallas_call | solution.py:334
  209.7 0.0 copy-start.1
  209.7 2.8 %copy.11 = bf16[1,512,1536]{2,1,0:T(8,128)(2,1)} copy(bf16[1,512,1536]{2,1,0:T(8,128)(2,1)} %get-tuple-element.12) | data formatting | bytes 3145728
  212.5 0.0 copy-done.1
  212.5 0.0 copy-start
  212.5 1.1 copy.12
  213.7 0.8 copy-done
  214.5 1.1 copy.13
Async XLA Ops:
  209.7 2.8 %copy-start.1 = (bf16[1,512,1536]{2,1,0:T(8,128)(2,1)S(1)}, bf16[1,512,1536]{2,1,0:T(8,128)(2,1)}, u32[]{:S(2)}) copy-start(bf16[1,512,1536]{2,1,0:T(8,128)(2,1)} %get-tuple-element.13) | copy-start | bytes 4718596
  212.5 2.0 copy-start

commit v3 on v2

--- a/solution.py
+++ b/solution.py
@@ -94,6 +94,12 @@
     def slot_b(m):
         return jnp.where(near, m % 2, 1)
 
+    def hidden_f(k):
+        return jnp.where(near, k % 3, 0)
+
+    def hidden_w(m):
+        return jnp.where(near, m % 3, 1 + m % 2)
+
     def put_away(k, c):
         return (pltpu.make_async_copy(act.at[0, c], far_act.at[k, c], sem_far.at[c]),
                 pltpu.make_async_copy(hidden.at[0, rows(c)], far_hid.at[k, rows(c)], sem_hfar.at[c]))
@@ -102,7 +108,7 @@
         return pltpu.make_async_copy(far_act.at[m, c], act.at[1, c], sem_near.at[c])
 
     def fetch_hidden(m):
-        return pltpu.make_async_copy(far_hid.at[m], hidden.at[1], sem_hnear.at[0])
+        return pltpu.make_async_copy(far_hid.at[m], hidden.at[1 + m % 2], sem_hnear.at[m % 2])
 
     def silu_parts(g, u):
         half = 0.5 * g
@@ -111,7 +117,7 @@
         return half + q, u * ((0.5 * z + 0.5) * ((half - q) + 1.0))
 
     def work_forward(k, c):
-        slot = slot_f(k)
+        slot, slot_h = slot_f(k), hidden_f(k)
         wide = ahead[k, rows(c), :].astype(F32)
         a_blk[...] = (wide * scale_of(wide)).astype(BF16)
         for n in range(0, ff, TILE):
@@ -120,24 +126,29 @@
             t, v = silu_parts(g, u)
             act[slot, c, :, n:n + TILE] = t
             act[slot, c, :, ff + n:ff + n + TILE] = v
-            hidden[slot, rows(c), n:n + TILE] = (t * u).astype(BF16)
-        y = rounded(dot(hidden[slot, rows(c), :], wd[...]))
+            hidden[slot_h, rows(c), n:n + TILE] = (t * u).astype(BF16)
+        y = rounded(dot(hidden[slot_h, rows(c), :], wd[...]))
         send_a[k % 2, rows(c), :] = (ahead[k, rows(c), :].astype(F32) + y).astype(BF16)
 
     def by_hidden(m, c):
-        slot = slot_b(m)
+        slot, keep = slot_b(m), m % 2
         for n in range(0, ff, TILE):
             dh = rounded(dot(behind[m, rows(c), :], wdt[:, n:n + TILE]))
-            dup[rows(c), n:n + TILE] = (dh * act[slot, c, :, n:n + TILE]).astype(BF16)
-            dgate[rows(c), n:n + TILE] = (dh * act[slot, c, :, ff + n:ff + n + TILE]).astype(BF16)
-
-    def by_input(m, c):
-        da = rounded(rounded(dot(dup[rows(c), :], wut[...])) + rounded(dot(dgate[rows(c), :], wgt[...])))
+            dup[keep, rows(c), n:n + TILE] = (dh * act[slot, c, :, n:n + TILE]).astype(BF16)
+            dgate[keep, rows(c), n:n + TILE] = (dh * act[slot, c, :, ff + n:ff + n + TILE]).astype(BF16)
+
+    def by_input(m, c, keep, send):
+        if send:
+            da = rounded(rounded(dot(dup[keep, rows(c), :], wut[...])) + rounded(dot(dgate[keep, rows(c), :], wgt[...])))
         wide = ahead[m, rows(c), :].astype(F32)
         scale = scale_of(wide)
-        inner = jnp.sum(da * wide, -1, keepdims=True)
-        by_norm = rounded(da * scale + (inner * (scale * scale * scale) * (-1.0 / width)) * wide)
-        send_b[m % 2, rows(c), :] = (behind[m, rows(c), :].astype(F32) + by_norm).astype(BF16)
+        normed = wide * scale
+        at[keep, :, rows(c)] = normed.astype(BF16).T
+        dyt[keep, :, rows(c)] = behind[m, rows(c), :].T
+        if send:
+            inner = jnp.sum(da * wide, -1, keepdims=True)
+            by_norm = rounded(da * scale + (inner * (scale * scale * scale) * (-1.0 / width)) * wide)
+            send_b[m % 2, rows(c), :] = (behind[m, rows(c), :].astype(F32) + by_norm).astype(BF16)
 
     def work_last(k, c):
         wide = ahead[k, rows(c), :].astype(F32)
@@ -147,19 +158,22 @@
             u = dot(a_blk[...], wu[:, n:n + TILE])
             dh = rounded(dot(behind[k, rows(c), :], wdt[:, n:n + TILE]))
             t, v = silu_parts(g, u)
-            hidden[0, rows(c), n:n + TILE] = (t * u).astype(BF16)
-            dup[rows(c), n:n + TILE] = (dh * t).astype(BF16)
-            dgate[rows(c), n:n + TILE] = (dh * v).astype(BF16)
-        by_input(k, c)
-
-    def weights(m, slot):
-        wide = ahead[m].astype(F32)
-        at[...] = (wide * scale_of(wide)).astype(BF16).T
-        dyt[...] = behind[m].T
+            hidden[k % 2, rows(c), n:n + TILE] = (t * u).astype(BF16)
+            dup[k % 2, rows(c), n:n + TILE] = (dh * t).astype(BF16)
+            dgate[k % 2, rows(c), n:n + TILE] = (dh * v).astype(BF16)
+        by_input(k, c, k % 2, True)
+
+    def weights(keep, slot):
         for n in range(0, ff, TILE):
-            tot_g[:, n:n + TILE] += rounded(dot(at[...], dgate[:, n:n + TILE]))
-            tot_u[:, n:n + TILE] += rounded(dot(at[...], dup[:, n:n + TILE]))
-            tot_d[:, n:n + TILE] += rounded(dot(dyt[...], hidden[slot, :, n:n + TILE]))
+            tot_g[:, n:n + TILE] += rounded(dot(at[keep], dgate[keep, :, n:n + TILE]))
+            tot_u[:, n:n + TILE] += rounded(dot(at[keep], dup[keep, :, n:n + TILE]))
+            tot_d[:, n:n + TILE] += rounded(dot(dyt[keep], hidden[slot, :, n:n + TILE]))
+
+    def weights_part(keep, slot, c):
+        part = pl.ds(pl.multiple_of(c * (width // CUTS), width // CUTS), width // CUTS)
+        tot_g[part, :] += rounded(dot(at[keep, part, :], dgate[keep]))
+        tot_u[part, :] += rounded(dot(at[keep, part, :], dup[keep]))
+        tot_d[part, :] += rounded(dot(dyt[keep, part, :], hidden[slot]))
 
     def before_forward(k, c):
         take_x(k, c).wait()
@@ -216,59 +230,78 @@
                     work_forward(k, c)
                     after_forward(k, c)
 
-            @pl.when((m >= 0) & (k < micro))
+            @pl.when((m >= 0) & (m < micro) & ~near)
+            def _():
+                fetch_hidden(m).start()
+
+            @pl.when((m >= 1) & ~near)
+            def _():
+                fetch_hidden(m - 1).wait()
+
+            def fetch_next(c):
+                @pl.when((m + 1 < micro) & ~near)
+                def _():
+                    fetch(m + 1, c).start()
+
+            def both(c):
+                before_backward(m, c, send)
+                before_forward(k, c)
+                work_forward(k, c)
+                by_hidden(m, c)
+                by_input(m, c, m % 2, send)
+
+            def both_sent(c):
+                if send:
+                    pass_back(m, c).start()
+                after_forward(k, c)
+                fetch_next(c)
+
+            @pl.when(m == 0)
             def _():
                 @each
                 def _(c):
-                    before_backward(m, c, send)
-                    before_forward(k, c)
-                    work_forward(k, c)
-                    by_hidden(m, c)
-                    if send:
-                        by_input(m, c)
-                        pass_back(m, c).start()
-                    after_forward(k, c)
+                    both(c)
+                    both_sent(c)
+
+            @pl.when((m >= 1) & (k < micro))
+            def _():
+                keep, slot = (m - 1) % 2, hidden_w(m - 1)
+
+                @each
+                def _(c):
+                    both(c)
+                    weights_part(keep, slot, c)
+                    both_sent(c)
+
+            @pl.when((k == micro) & ~near)
+            def _():
+                @each
+                def _(c):
+                    for copy in put_away(micro - 1, c):
+                        copy.wait()
 
             @pl.when(k >= micro)
             def _():
+                weights((m - 1) % 2, hidden_w(m - 1))
+
                 @each
                 def _(c):
                     before_backward(m, c, send)
                     by_hidden(m, c)
+                    by_input(m, c, m % 2, send)
                     if send:
-                        by_input(m, c)
                         pass_back(m, c).start()
-
-            @pl.when((k == micro) & ~near)
-            def _():
-                @each
-                def _(c):
-                    for copy in put_away(micro - 1, c):
-                        copy.wait()
-
-            coming = (m + 1 >= 0) & (m + 1 < micro) & ~near
-
-            @pl.when(coming)
-            def _():
-                each(lambda c: fetch(m + 1, c).start())
+                    fetch_next(c)
+
+            @pl.when((m == -1) & ~near)
+            def _():
+                each(lambda c: fetch(0, c).start())
 
             @pl.when(k == 0)
             def _():
                 turn()
                 clear()
 
-            @pl.when(m >= 0)
-            def _():
-                @pl.when(~near)
-                def _():
-                    fetch_hidden(m).wait()
-
-                weights(m, slot_b(m))
-
-            @pl.when(coming)
-            def _():
-                fetch_hidden(m + 1).start()
-
     for load in loads:
         load.wait()
 
@@ -285,29 +318,42 @@
         turn()
         clear()
 
-        @pl.loop(0, micro)
+        def block(k, c, part):
+            take_x(k, c).wait()
+            take_dy(k, c).wait()
+
+            @pl.when(k >= 2)
+            def _():
+                pass_back(k, c).wait_send()
+
+            work_last(k, c)
+            if part:
+                weights_part((k - 1) % 2, (k - 1) % 2, c)
+            pass_back(k, c).start()
+
+        each(lambda c: block(0, c, False))
+
+        @pl.loop(1, micro)
         def _(k):
-            @each
-            def _(c):
-                take_x(k, c).wait()
-                take_dy(k, c).wait()
-
-                @pl.when(k >= 2)
-                def _():
-                    pass_back(k, c).wait_send()
-
-                work_last(k, c)
-                pass_back(k, c).start()
-
-            weights(k, 0)
-
-    dgate[...] = tot_g[...].astype(BF16)
+            each(lambda c: block(k, c, True))
+
+    @pl.when((me < last) & ~near)
+    def _():
+        fetch_hidden(micro - 1).wait()
+
+    keep = (micro - 1) % 2
+    spare = 1 - keep
+    slot = jnp.where(me == last, keep, hidden_w(micro - 1))
     stores = [pltpu.make_async_copy(src, dst.at[0], sem_out.at[i])
-              for i, (src, dst) in enumerate(((dgate, out_gate), (dup, out_up), (wd, out_down)))]
+              for i, (src, dst) in enumerate(((dgate.at[spare], out_gate), (dup.at[spare], out_up), (wd, out_down)))]
+    for n in range(0, ff, TILE):
+        dgate[spare, :, n:n + TILE] = (tot_g[:, n:n + TILE] + rounded(dot(at[keep], dgate[keep, :, n:n + TILE]))).astype(BF16)
     stores[0].start()
-    dup[...] = tot_u[...].astype(BF16)
+    for n in range(0, ff, TILE):
+        dup[spare, :, n:n + TILE] = (tot_u[:, n:n + TILE] + rounded(dot(at[keep], dup[keep, :, n:n + TILE]))).astype(BF16)
     stores[1].start()
-    wd[...] = tot_d[...].astype(BF16).T
+    for n in range(0, ff, TILE):
+        wd[n:n + TILE, :] = (tot_d[:, n:n + TILE] + rounded(dot(dyt[keep], hidden[slot, :, n:n + TILE]))).astype(BF16).T
     stores[2].start()
 
     @pl.when(me < last)
@@ -344,13 +390,13 @@
                 vmem((ff, width), BF16), vmem((ff, width), BF16), vmem((width, ff), BF16),
                 vmem(x.shape, BF16), vmem(x.shape, BF16),
                 vmem((2, tokens, width), BF16), vmem((2, tokens, width), BF16),
-                vmem((2, CUTS, rows_n, 2 * ff), F32), vmem((2, tokens, ff), BF16),
-                vmem((tokens, ff), BF16), vmem((tokens, ff), BF16),
-                vmem((width, tokens), BF16), vmem((width, tokens), BF16),
+                vmem((2, CUTS, rows_n, 2 * ff), F32), vmem((3, tokens, ff), BF16),
+                vmem((2, tokens, ff), BF16), vmem((2, tokens, ff), BF16),
+                vmem((2, width, tokens), BF16), vmem((2, width, tokens), BF16),
                 vmem((width, ff), F32), vmem((width, ff), F32), vmem((width, ff), F32),
                 vmem((rows_n, width), BF16),
                 dma((3,)), dma((micro, CUTS)), dma((micro, CUTS)), dma((2, CUTS)), dma((2, CUTS)),
-                dma((CUTS,)), dma((CUTS,)), dma((CUTS,)), dma((1,)), dma((3,)),
+                dma((CUTS,)), dma((CUTS,)), dma((CUTS,)), dma((2,)), dma((3,)),
             ],
             compiler_params=pltpu.CompilerParams(collective_id=0, has_side_effects=True, vmem_limit_bytes=67_000_000),
             name="pipeline",

time: 216 us -> 208 us (0.963)
  Pallas kernels: 209 us -> 201 us
    pallas_call x1, Pallas kernels: 209 us -> 201 us  [step(): pl.pallas_call(kernel, out_shape=(jax.ShapeDtypeStruct((1, width, ff), BF...]
where the time goes in v3:
time: 208 us
  Pallas kernels  201 us (97%)
  local copies, waits for them, and re-layouts  5.89 us (3%)
    pallas_call x1, Pallas kernels, step(): pl.pallas_call(kernel, out_shape=(jax.ShapeDtypeStruct((1, width, ff), BF...  201 us
    unnamed x7, local copies, waits for them, and re-layouts  5.89 us

profile of v3, /device:TPU:2, one launch (start us, length us, event | category | flops | bytes accessed | tf_op | source)
XLA Modules:
  0.0 207.8 jit_solution(10566507918903669006)
XLA Ops:
  0.6 201.2 %pipeline.1 = (bf16[1,512,1536]{2,1,0:T(8,128)(2,1)}, bf16[1,512,1536]{2,1,0:T(8,128)(2,1)}, bf16[1,1536,512]{2,1,0:T(8,128)(2,1)}, f32[16,4,128,3072]{3,2,1,0:T(8,128)}, bf16[16,512,1536]{2,1,0:T(8,128)(2,1)}) custom-call(bf16[16,512,512]{2,1,0:T(8,128)(2,1)} %x.1, bf16[16,512,512]{2,1,0:T(8,128)(2,1)} %dy.1, bf16[1,512,1536]{2,1,0:T(8,128)(2,1)} %w_gate.1, ...), custom_call_target="tpu_custom_call" | custom-call | tf_op jit(solution)/shard_map/pipeline/pallas_call | solution.py:380
  201.9 0.0 copy-start.1
  201.9 2.8 %copy.11 = bf16[1,512,1536]{2,1,0:T(8,128)(2,1)} copy(bf16[1,512,1536]{2,1,0:T(8,128)(2,1)} %get-tuple-element.12) | data formatting | bytes 3145728
  204.7 0.0 copy-done.1
  204.7 0.0 copy-start
  204.7 1.1 copy.12
  205.8 0.8 copy-done
  206.6 1.1 copy.13
Async XLA Ops:
  201.9 2.8 %copy-start.1 = (bf16[1,512,1536]{2,1,0:T(8,128)(2,1)S(1)}, bf16[1,512,1536]{2,1,0:T(8,128)(2,1)}, u32[]{:S(2)}) copy-start(bf16[1,512,1536]{2,1,0:T(8,128)(2,1)} %get-tuple-element.13) | copy-start | bytes 4718596
  204.7 2.0 copy-start

commit v4 on v3

--- a/solution.py
+++ b/solution.py
@@ -244,8 +244,6 @@
                     fetch(m + 1, c).start()
 
             def both(c):
-                before_backward(m, c, send)
-                before_forward(k, c)
                 work_forward(k, c)
                 by_hidden(m, c)
                 by_input(m, c, m % 2, send)
@@ -260,6 +258,8 @@
             def _():
                 @each
                 def _(c):
+                    before_backward(m, c, send)
+                    before_forward(k, c)
                     both(c)
                     both_sent(c)
 
@@ -269,9 +269,32 @@
 
                 @each
                 def _(c):
+                    take_x(k, c).wait()
+                    take_dy(m, c).wait()
+                    pass_on(k, c).wait_send()
+
+                    @pl.when(~near)
+                    def _():
+                        fetch(m, c).wait()
+                        for copy in put_away(k - 1, c):
+                            copy.wait()
+
+                    if send:
+                        @pl.when(m >= 2)
+                        def _():
+                            pass_back(m, c).wait_send()
+
                     both(c)
                     weights_part(keep, slot, c)
-                    both_sent(c)
+                    if send:
+                        pass_back(m, c).start()
+                    pass_on(k, c).start()
+
+                    @pl.when(~near)
+                    def _():
+                        for copy in put_away(k, c):
+                            copy.start()
+                        fetch(m + 1, c).start()
 
             @pl.when((k == micro) & ~near)
             def _():

time: 208 us -> 208 us (level)
  no operation moved by 1% of the time
where the time goes in v4:
time: 208 us
  Pallas kernels  201 us (97%)
  local copies, waits for them, and re-layouts  5.89 us (3%)
    pallas_call x1, Pallas kernels, step(): pl.pallas_call(kernel, out_shape=(jax.ShapeDtypeStruct((1, width, ff), BF...  201 us
    unnamed x7, local copies, waits for them, and re-layouts  5.89 us

profile of v4, /device:TPU:2, one launch (start us, length us, event | category | flops | bytes accessed | tf_op | source)
XLA Modules:
  0.0 207.8 jit_solution(15714093080362509866)
XLA Ops:
  0.6 201.3 %pipeline.1 = (bf16[1,512,1536]{2,1,0:T(8,128)(2,1)}, bf16[1,512,1536]{2,1,0:T(8,128)(2,1)}, bf16[1,1536,512]{2,1,0:T(8,128)(2,1)}, f32[16,4,128,3072]{3,2,1,0:T(8,128)}, bf16[16,512,1536]{2,1,0:T(8,128)(2,1)}) custom-call(bf16[16,512,512]{2,1,0:T(8,128)(2,1)} %x.1, bf16[16,512,512]{2,1,0:T(8,128)(2,1)} %dy.1, bf16[1,512,1536]{2,1,0:T(8,128)(2,1)} %w_gate.1, ...), custom_call_target="tpu_custom_call" | custom-call | tf_op jit(solution)/shard_map/pipeline/pallas_call | solution.py:403
  201.9 0.0 copy-start.1
  201.9 2.8 %copy.11 = bf16[1,512,1536]{2,1,0:T(8,128)(2,1)} copy(bf16[1,512,1536]{2,1,0:T(8,128)(2,1)} %get-tuple-element.12) | data formatting | bytes 3145728
  204.7 0.0 copy-done.1
  204.7 0.0 copy-start
  204.7 1.1 copy.12
  205.8 0.8 copy-done
  206.7 1.1 copy.13
Async XLA Ops:
  201.9 2.8 %copy-start.1 = (bf16[1,512,1536]{2,1,0:T(8,128)(2,1)S(1)}, bf16[1,512,1536]{2,1,0:T(8,128)(2,1)}, u32[]{:S(2)}) copy-start(bf16[1,512,1536]{2,1,0:T(8,128)(2,1)} %get-tuple-element.13) | copy-start | bytes 4718596
  204.7 2.0 copy-start
